TPU v7x, 256 devices: a whole 4x4x8 slice. The times are simulated.
256 devices in a mesh: gz: 64 (over x, z, core), gy: 4 (over y).
Axes of the slice: x: 4, y: 4, z: 8, core: 2. Of those that a mesh axis runs over, the one named last changes fastest.
Arguments:
- source_first: float32 [512, 32, 16, 128], P('gz', 'gy'), may hold values from -6 to 6
- source_second: float32 [256, 16, 16, 128], P('gz', 'gy'), may hold values from -6 to 6
- source_third: float32 [128, 8, 16, 128], P('gz', 'gy'), may hold values from -6 to 6
- source_fourth: float32 [64, 4, 16, 128], P('gz', 'gy'), may hold values from -6 to 6
- guess_first: float32 [512, 32, 16, 128], P('gz', 'gy'), may hold values from -6 to 6
- guess_second: float32 [256, 16, 16, 128], P('gz', 'gy'), may hold values from -6 to 6
- guess_third: float32 [128, 8, 16, 128], P('gz', 'gy'), may hold values from -6 to 6
- guess_fourth: float32 [64, 4, 16, 128], P('gz', 'gy'), may hold values from -6 to 6
- shift_first: float32 [512, 32, 128], P('gz', 'gy'), may hold values from 0.2 to 2
- shift_second: float32 [256, 16, 128], P('gz', 'gy'), may hold values from 0.2 to 2
- shift_third: float32 [128, 8, 128], P('gz', 'gy'), may hold values from 0.2 to 2
- shift_fourth: float32 [64, 4, 128], P('gz', 'gy'), may hold values from 0.2 to 2
- blocks_first: bfloat16 [512, 32, 2, 128, 128], P('gz', 'gy'), may hold values from -0.375 to 0.375
- blocks_second: bfloat16 [256, 16, 2, 128, 128], P('gz', 'gy'), may hold values from -0.375 to 0.375
- blocks_third: bfloat16 [128, 8, 2, 128, 128], P('gz', 'gy'), may hold values from -0.375 to 0.375
- links_first: int32 [512, 32, 2], P('gz', 'gy'), may hold values from 0 to 4095, as said below
- links_second: int32 [256, 16, 2], P('gz', 'gy'), may hold values from 0 to 1023, as said below
- links_third: int32 [128, 8, 2], P('gz', 'gy'), may hold values from 0 to 255, as said below
Outputs:
- smooth_first: float32 [512, 32, 16, 128], P('gz', 'gy')
- smooth_second: float32 [256, 16, 16, 128], P('gz', 'gy')
- smooth_third: float32 [128, 8, 16, 128], P('gz', 'gy')
- smooth_fourth: float32 [64, 4, 16, 128], P('gz', 'gy')
Inputs may be any that keep to these rules, and one draw needn't show every extreme that they name: `links_first`: entry k of fine cell (i, j) names coarse column x * 16 + y with x within one of i // 2 and y within one of j // 2, both periodic on the coarse grid. `links_second`: entry k of cell (i, j) names coarse column x * 8 + y with x within one of i // 2 and y within one of j // 2, both periodic on the coarse grid. `links_third`: entry k of cell (i, j) names coarse column x * 4 + y with x within one of i // 2 and y within one of j // 2, both periodic on the coarse grid.
All inputs are finite; a program needn't handle non-finite values.
Results may differ from a plain program's by a relative error of at most 0.0005.
Values may be sent and summed in bfloat16 or wider, within the bound.
A program may use at most 256 MiB of HBM per device.

v0:
```python
import functools

import jax
import jax.numpy as jnp
from jax import lax
from jax.experimental import pallas as pl
from jax.experimental.pallas import tpu as pltpu
from jax.sharding import PartitionSpec as P

MESH = pl.DeviceIdType.MESH

upper_edge = 14.0
lower_edge = upper_edge / 8.0
CENTRE = (upper_edge + lower_edge) / 2.0
HALF = (upper_edge - lower_edge) / 2.0
RATIO = CENTRE / HALF
FACTOR_0 = 1.0 / RATIO
FACTOR_1 = 1.0 / (2.0 * RATIO - FACTOR_0)
FACTOR_2 = 1.0 / (2.0 * RATIO - FACTOR_1)
A2, B2 = FACTOR_1 * FACTOR_0, 2.0 * FACTOR_1 / HALF
A3, B3 = FACTOR_2 * FACTOR_1, 2.0 * FACTOR_2 / HALF

RADIUS = 3
RINGS = (0, 0, 0, 0)


class Level:
    def __init__(self, nz, ny, peers_z, peers_y, ring):
        self.nz, self.ny, self.ring = nz, ny, ring
        self.peers_y = peers_y
        self.halo = RADIUS + ring
        self.total_y = ny * peers_y
        self.full = ny + 2 * self.halo >= self.total_y
        self.rows = nz + 2 * self.halo
        self.cols = self.total_y if self.full else ny + 2 * self.halo
        self.off = 0 if self.full else self.halo

    def col(self, y):
        return y % self.total_y if self.full else y + self.off

    def needed(self, z, y, radius):
        def gap(p, n):
            return max(0, -p - self.ring, p - (n - 1) - self.ring)

        turns = (-1, 0, 1) if self.full else (0,)
        gap_y = min(gap(y + t * self.total_y, self.ny) for t in turns)
        return gap(z, self.nz) + gap_y <= radius

    def messages(self, radius):
        found = []
        reach = -(-self.halo // self.nz)
        offsets_y = range(-(self.peers_y // 2 - 1), self.peers_y // 2 + 1) if self.full else range(-1, 2)
        for oz in range(-reach, reach + 1):
            for oy in offsets_y:
                if (oz, oy) == (0, 0):
                    continue
                spans = []
                for i in range(self.nz):
                    js = [j for j in range(self.ny) if self.needed(i - oz * self.nz, j - oy * self.ny, radius)]
                    if not js:
                        continue
                    span = (js[0], len(js))
                    if spans and spans[-1][1] == span:
                        spans[-1][2] += 1
                    else:
                        spans.append([i, span, 1])
                for i, (j, count), rows in spans:
                    found.append((oz, oy, i, j, rows, count))
        return found


def ring_messages(nz, ny):
    found = []
    for oz in (-1, 0, 1):
        for oy in (-1, 0, 1):
            if (oz, oy) == (0, 0):
                continue
            i, rows = (0, nz) if oz == 0 else ((nz - 1, 1) if oz == 1 else (0, 1))
            j, count = (0, ny) if oy == 0 else ((ny - 1, 1) if oy == 1 else (0, 1))
            found.append((oz, oy, i, j, rows, count))
    return found


def plan(shapes, peers_z, peers_y):
    levels = [Level(nz, ny, peers_z, peers_y, ring) for (nz, ny), ring in zip(shapes, RINGS)]
    table = []
    for number, level in enumerate(levels):
        for kind, radius in (("u", RADIUS), ("f", RADIUS - 1), ("t", RADIUS - 1)):
            table += [(kind, number, m) for m in level.messages(radius)]
        if number < len(levels) - 1 and level.ring == 0:
            table += [("c", number, m) for m in ring_messages(level.nz, level.ny)]
    return levels, table


def rolls(v):
    return pltpu.roll(v, 1, 1) + pltpu.roll(v, v.shape[1] - 1, 1)


def kernel(levels, table, peers, *refs):
    n = len(levels)
    source, guess, shift = refs[0:n], refs[n : 2 * n], refs[2 * n : 3 * n]
    refs = refs[3 * n :]
    blocks, links = (None,) + refs[: n - 1], (None,) + refs[n - 1 : 2 * n - 2]
    refs = refs[2 * n - 2 :]
    outs, refs = refs[:n], refs[n:]
    u, f, t, d1, d2 = (refs[k * n : (k + 1) * n] for k in range(5))
    refs = refs[5 * n :]
    g, b, c = (None,) + refs[: n - 1], (None,) + refs[n - 1 : 2 * n - 2], refs[2 * n - 2 : 3 * n - 3]
    result = refs[3 * n - 3 : 4 * n - 3]
    local_sem, out_sem, send_sem, recv_sem = refs[4 * n - 3 :]

    peers_z, peers_y = peers
    my_z, my_y = lax.axis_index("gz"), lax.axis_index("gy")

    def peer(oz, oy):
        return (lax.rem(my_z + (oz + peers_z), peers_z), lax.rem(my_y + (oy + peers_y), peers_y))

    barrier = pltpu.get_barrier_semaphore()
    partners = sorted({m[:2] for _, _, m in table})
    for oz, oy in partners:
        pl.semaphore_signal(barrier, inc=1, device_id=peer(oz, oy), device_id_type=MESH)

    loads = {}

    def load(key, src, dst):
        loads[key] = pltpu.make_async_copy(src, dst, local_sem.at[len(loads)])
        loads[key].start()

    for number, level in enumerate(levels):
        own = (pl.ds(level.halo, level.nz), pl.ds(level.off, level.ny))
        load(("f", number), source[number], f[number].at[own])
        load(("t", number), shift[number], t[number].at[own])
        if number == 0:
            load(("g", 0), guess[0], u[0].at[own])
    for number in range(1, n):
        load(("g", number), guess[number], g[number])
        load(("b", number), blocks[number], b[number])

    buffers = {"u": u, "f": f, "t": t, "c": c}
    copies = {}

    def describe(index):
        kind, number, (oz, oy, i, j, rows, count) = table[index]
        level, ref = levels[number], buffers[kind][number]
        zi, yj = i - oz * level.nz, j - oy * level.ny
        if kind == "c":
            source_at = (pl.ds(1 + i, rows), pl.ds(1 + j, count))
            target_at = (pl.ds(1 + zi, rows), pl.ds(1 + yj, count))
        else:
            source_at = (pl.ds(level.halo + i, rows), pl.ds(level.col(j), count))
            target_at = (pl.ds(level.halo + zi, rows), pl.ds(level.col(yj), count))
        return pltpu.make_async_remote_copy(
            src_ref=ref.at[source_at],
            dst_ref=ref.at[target_at],
            send_sem=send_sem.at[index],
            recv_sem=recv_sem.at[index],
            device_id=peer(oz, oy),
            device_id_type=MESH,
        )

    def send(kind, number):
        for index, (k, l, _) in enumerate(table):
            if (k, l) == (kind, number):
                copies[index] = describe(index)
                copies[index].start()

    def receive(kind, number):
        for index, (k, l, _) in enumerate(table):
            if (k, l) == (kind, number):
                copies[index].wait_recv()

    def sweep(level, ring, body):
        def row(z, carry):
            if level.full:
                cells = range(level.cols)
            else:
                cells = range(level.off - ring, level.off + level.ny + ring)
            for y in cells:
                body(z, y)
            return carry

        lax.fori_loop(level.halo - ring, level.halo + level.nz + ring, row, 0)

    def beside(level, ref, z, y, middle):
        up, down = ((y + 1) % level.cols, (y - 1) % level.cols) if level.full else (y + 1, y - 1)
        return ref[z - 1, y] + ref[z + 1, y] + ref[z, up] + ref[z, down] + rolls(middle)

    def smooth(number):
        level = levels[number]
        uu, ff, tt, p, q = u[number], f[number], t[number], d1[number], d2[number]
        ring = level.ring

        def first(z, y):
            v = uu[z, y]
            p[z, y] = (ff[z, y] - ((6.0 + tt[z, y]) * v - beside(level, uu, z, y, v))) * (1.0 / CENTRE)

        def second(z, y):
            v = p[z, y]
            q[z, y] = ((A2 + B2 * CENTRE) - B2 * (6.0 + tt[z, y])) * v + B2 * beside(level, p, z, y, v)

        def third(z, y):
            v, w = q[z, y], p[z, y]
            out = uu[z, y] + (1.0 - B3 * A2 / B2) * w
            out = out + ((1.0 + A3 + B3 / B2) - B3 * (6.0 + tt[z, y])) * v + B3 * beside(level, q, z, y, v)
            finish(z, y, out)

        def finish(z, y, out):
            at = y - level.off
            if 0 <= at < level.ny:
                if ring == 0:
                    result[number][z - level.halo, at] = out
                    if number < n - 1:
                        c[number][z - level.halo + 1, at + 1] = out.astype(jnp.bfloat16)
                else:
                    result[number][z - level.halo + ring, at] = out
            if ring:
                for turn in (0, level.total_y if level.full else 0):
                    col = at + 1 - turn
                    if 0 <= col < level.ny + 2:
                        c[number][z - level.halo + 1, col] = out.astype(jnp.bfloat16)
                        break

        sweep(level, ring + 2, first)
        sweep(level, ring + 1, second)
        if level.full:
            wanted = sorted({y % level.total_y for y in range(-ring, level.ny + ring)})
        else:
            wanted = range(level.off - ring, level.off + level.ny + ring)

        def row(z, carry):
            for y in wanted:
                third(z, y)
            return carry

        lax.fori_loop(level.halo - ring, level.halo + level.nz + ring, row, 0)
        own = result[number] if ring == 0 else result[number].at[pl.ds(ring, level.nz)]
        out_copy = pltpu.make_async_copy(own, outs[number], out_sem.at[number])
        out_copy.start()
        return out_copy

    def prolong(number):
        level, coarse = levels[number], levels[number - 1]
        full_cols = coarse.ny * peers_y
        full_rows = coarse.nz * peers_z
        base_row = my_z * coarse.nz - 1
        base_col = my_y * coarse.ny - 1

        def row(i, carry):
            for j in range(level.ny):
                total = g[number][i, j]
                for k in range(2):
                    link = links[number][(i, j, k) if level.ny == 2 else (i, k, j)]
                    at_row = lax.rem(link // full_cols - base_row + full_rows, full_rows)
                    at_col = lax.rem(lax.rem(link, full_cols) - base_col + full_cols, full_cols)
                    total = total + lax.dot_general(
                        c[number - 1][jnp.minimum(at_row, coarse.nz + 1), jnp.minimum(at_col, coarse.ny + 1)],
                        b[number][i, j, k],
                        (((1,), (1,)), ((), ())),
                        preferred_element_type=jnp.float32,
                    )
                u[number][level.halo + i, level.off + j] = total
            return carry

        lax.fori_loop(0, level.nz, row, 0)

    for key in (("f", 0), ("t", 0), ("g", 0)):
        loads[key].wait()
    pl.semaphore_wait(barrier, len(partners))
    for kind in ("u", "f", "t"):
        send(kind, 0)
    for number in range(1, n):
        for kind in ("f", "t"):
            loads[(kind, number)].wait()
            send(kind, number)
    outputs = []
    for number in range(n):
        if number:
            loads[("g", number)].wait()
            loads[("b", number)].wait()
            prolong(number)
            send("u", number)
        for kind in ("f", "t", "u"):
            receive(kind, number)
        outputs.append(smooth(number))
        if number < n - 1 and levels[number].ring == 0:
            send("c", number)
            receive("c", number)
    for index in range(len(table)):
        copies[index].wait_send()
    for copy in outputs:
        copy.wait()


def shards(peers, *arrays):
    fine_to_coarse = lambda group: group[::-1]
    source, guess, shift = (fine_to_coarse(arrays[k : k + 4]) for k in (0, 4, 8))
    blocks, links = (fine_to_coarse(arrays[k : k + 3]) for k in (12, 15))
    n = len(source)
    sides, line = source[0].shape[2:]
    levels, table = plan([x.shape[:2] for x in source], *peers)
    shift = [x.reshape(x.shape[0], x.shape[1], 1, line) for x in shift]
    links = [x if x.shape[1] == x.shape[2] else x.transpose(0, 2, 1) for x in links]
    f32, bf16 = jnp.float32, jnp.bfloat16
    extended = [pltpu.VMEM((l.rows, l.cols, sides, line), f32) for l in levels]
    scratch = extended + extended + [pltpu.VMEM((l.rows, l.cols, 1, line), f32) for l in levels] + extended + extended
    scratch += [pltpu.VMEM(x.shape, f32) for x in guess[1:]]
    scratch += [pltpu.VMEM(x.shape, bf16) for x in blocks]
    scratch += [pltpu.VMEM((l.nz + 2, l.ny + 2, sides, line), bf16) for l in levels[:-1]]
    scratch += [pltpu.VMEM((l.nz + 2 * l.ring, l.ny, sides, line), f32) for l in levels]
    scratch += [
        pltpu.SemaphoreType.DMA((3 * n + 2 * (n - 1),)),
        pltpu.SemaphoreType.DMA((n,)),
        pltpu.SemaphoreType.DMA((len(table),)),
        pltpu.SemaphoreType.DMA((len(table),)),
    ]
    hbm = pl.BlockSpec(memory_space=pltpu.HBM)
    results = pl.pallas_call(
        functools.partial(kernel, levels, table, peers),
        out_shape=[jax.ShapeDtypeStruct(x.shape, f32) for x in source],
        in_specs=[hbm] * (3 * n + len(blocks)) + [pl.BlockSpec(memory_space=pltpu.SMEM)] * len(links),
        out_specs=[hbm] * n,
        scratch_shapes=scratch,
        compiler_params=pltpu.CompilerParams(
            collective_id=0, has_side_effects=True, vmem_limit_bytes=67043328
        ),
    )(*source, *guess, *shift, *blocks, *links)
    return tuple(results[::-1])


def solution(mesh):
    wide = P("gz", "gy", None, None)
    flat = P("gz", "gy", None)
    in_specs = (wide,) * 8 + (flat,) * 4 + (P("gz", "gy", None, None, None),) * 3 + (flat,) * 3
    peers = (mesh.shape["gz"], mesh.shape["gy"])
    return jax.shard_map(
        functools.partial(shards, peers), mesh=mesh, in_specs=in_specs, out_specs=(wide,) * 4, check_vma=False
    )
```

profile of v0, /device:TPU:1, one launch (start us, length us, event | category | flops | bytes accessed | tf_op | source)
XLA Modules:
  0.0 73.1 jit_solution(10559847147083930742)
XLA Ops:
  0.6 66.3 %shard_map.201 = (f32[1,1,16,128]{3,2,1,0:T(8,128)}, f32[2,2,16,128]{3,2,1,0:T(8,128)}, f32[4,4,16,128]{3,2,1,0:T(8,128)}, f32[8,8,16,128]{3,2,1,0:T(8,128)}) custom-call(f32[1,1,16,128]{3,2,1,0:T(8,128)} %refs_0_.1, f32[2,2,16,128]{3,2,1,0:T(8,128)} %refs_1_.1, f32[4,4,16,128]{3,2,1,0:T(8,128)} %refs_2_.1, f32[8,8,16,128]{3,2,1,0:T(8,128)} %refs_3_.1, ...), custom_call_target="tpu_custom_call" | custom-call | tf_op jit(solution)/shard_map/pallas_call | solution.py:317
  67.0 1.9 %copy.26 = f32[8,8,16,128]{3,2,1,0:T(8,128)} copy(f32[8,8,16,128]{3,2,1,0:T(8,128)} %get-tuple-element.16) | data formatting | bytes 1048576
  68.8 1.6 %copy.27 = f32[4,4,16,128]{3,2,1,0:T(8,128)} copy(f32[4,4,16,128]{3,2,1,0:T(8,128)} %get-tuple-element.17) | data formatting | bytes 262144
  70.4 1.4 %copy.28 = f32[2,2,16,128]{3,2,1,0:T(8,128)} copy(f32[2,2,16,128]{3,2,1,0:T(8,128)} %get-tuple-element.18) | data formatting | bytes 65536
  71.8 1.3 %copy.29 = f32[1,1,16,128]{3,2,1,0:T(8,128)} copy(f32[1,1,16,128]{3,2,1,0:T(8,128)} %get-tuple-element.19) | data formatting | bytes 16384
where the time goes:
time: 73.4 us; the launch traced here: 73.1 us
  Pallas kernels  66.3 us (90%)
  local copies, waits for them, and re-layouts  6.1 us (8%)
    pallas_call x1, Pallas kernels, shards(): pl.pallas_call(functools.partial(kernel, levels, table, peers), out_shape...  66.3 us
    unnamed x4, local copies, waits for them, and re-layouts  6.1 us

commit v1 on v0

--- a/solution.py
+++ b/solution.py
@@ -22,6 +22,8 @@
 
 RADIUS = 3
 RINGS = (0, 0, 0, 0)
+STRAIGHT = 40
+ROWS = 2
 
 
 class Level:
@@ -34,6 +36,7 @@
         self.rows = nz + 2 * self.halo
         self.cols = self.total_y if self.full else ny + 2 * self.halo
         self.off = 0 if self.full else self.halo
+        self.cols_of_ring = sorted({self.col(y) for y in range(-ring, ny + ring)})
 
     def col(self, y):
         return y % self.total_y if self.full else y + self.off
@@ -92,6 +95,10 @@
     return levels, table
 
 
+def modulo(value, size):
+    return (value + size) & (size - 1) if size & (size - 1) == 0 else lax.rem(value + size, size)
+
+
 def rolls(v):
     return pltpu.roll(v, 1, 1) + pltpu.roll(v, v.shape[1] - 1, 1)
 
@@ -107,7 +114,9 @@
     refs = refs[5 * n :]
     g, b, c = (None,) + refs[: n - 1], (None,) + refs[n - 1 : 2 * n - 2], refs[2 * n - 2 : 3 * n - 3]
     result = refs[3 * n - 3 : 4 * n - 3]
-    local_sem, out_sem, send_sem, recv_sem = refs[4 * n - 3 :]
+    lines, refs = (None,) + refs[4 * n - 3 : 5 * n - 4], refs[5 * n - 4 :]
+    local_sem, out_sem, send_sem, recv_sem = refs
+    c_flat = [x.reshape((-1,) + x.shape[2:]) for x in c]
 
     peers_z, peers_y = peers
     my_z, my_y = lax.axis_index("gz"), lax.axis_index("gy")
@@ -169,17 +178,22 @@
             if (k, l) == (kind, number):
                 copies[index].wait_recv()
 
-    def sweep(level, ring, body):
-        def row(z, carry):
-            if level.full:
-                cells = range(level.cols)
-            else:
-                cells = range(level.off - ring, level.off + level.ny + ring)
-            for y in cells:
-                body(z, y)
-            return carry
-
-        lax.fori_loop(level.halo - ring, level.halo + level.nz + ring, row, 0)
+    def sweep(level, ring, body, after=None):
+        cols = sorted({level.col(y) for y in range(-ring, level.ny + ring)})
+        first, count = level.halo - ring, level.nz + 2 * ring
+        step = count if count * len(cols) <= STRAIGHT else ROWS
+
+        def rows(start):
+            for z in range(step):
+                for y in cols:
+                    body(start + z, y)
+            if after is not None:
+                after(start, step)
+
+        if step == count:
+            rows(first)
+        else:
+            lax.fori_loop(0, count // step, lambda i, carry: (rows(first + i * step), carry)[1], 0)
 
     def beside(level, ref, z, y, middle):
         up, down = ((y + 1) % level.cols, (y - 1) % level.cols) if level.full else (y + 1, y - 1)
@@ -205,64 +219,63 @@
             finish(z, y, out)
 
         def finish(z, y, out):
-            at = y - level.off
-            if 0 <= at < level.ny:
-                if ring == 0:
-                    result[number][z - level.halo, at] = out
-                    if number < n - 1:
-                        c[number][z - level.halo + 1, at + 1] = out.astype(jnp.bfloat16)
-                else:
-                    result[number][z - level.halo + ring, at] = out
-            if ring:
-                for turn in (0, level.total_y if level.full else 0):
-                    col = at + 1 - turn
-                    if 0 <= col < level.ny + 2:
-                        c[number][z - level.halo + 1, col] = out.astype(jnp.bfloat16)
-                        break
+            result[number][z - level.halo + ring, level.cols_of_ring.index(y)] = out
+            if number < n - 1:
+                at = (y - level.off + 1) % level.total_y if level.full else y - level.off + 1
+                c[number][z - level.halo + 1, at] = out.astype(jnp.bfloat16)
+
+        def copy_out(start, rows):
+            at = start - level.halo
+            own = result[number].at[pl.ds(at, rows)]
+            pltpu.make_async_copy(own, outs[number].at[pl.ds(at, rows)], out_sem.at[number]).start()
 
         sweep(level, ring + 2, first)
         sweep(level, ring + 1, second)
-        if level.full:
-            wanted = sorted({y % level.total_y for y in range(-ring, level.ny + ring)})
-        else:
-            wanted = range(level.off - ring, level.off + level.ny + ring)
-
-        def row(z, carry):
-            for y in wanted:
-                third(z, y)
-            return carry
-
-        lax.fori_loop(level.halo - ring, level.halo + level.nz + ring, row, 0)
-        own = result[number] if ring == 0 else result[number].at[pl.ds(ring, level.nz)]
-        out_copy = pltpu.make_async_copy(own, outs[number], out_sem.at[number])
-        out_copy.start()
-        return out_copy
-
-    def prolong(number):
+        sweep(level, ring, third, None if ring else copy_out)
+        own = result[number]
+        if ring:
+            own_cols = level.cols_of_ring.index(level.off)
+            own = own.at[pl.ds(ring, level.nz), pl.ds(own_cols, level.ny)]
+            pltpu.make_async_copy(own, outs[number], out_sem.at[number]).start()
+        return pltpu.make_async_copy(own, outs[number], out_sem.at[number])
+
+    def index_lines(number):
         level, coarse = levels[number], levels[number - 1]
-        full_cols = coarse.ny * peers_y
-        full_rows = coarse.nz * peers_z
         base_row = my_z * coarse.nz - 1
         base_col = my_y * coarse.ny - 1
 
         def row(i, carry):
             for j in range(level.ny):
-                total = g[number][i, j]
                 for k in range(2):
                     link = links[number][(i, j, k) if level.ny == 2 else (i, k, j)]
-                    at_row = lax.rem(link // full_cols - base_row + full_rows, full_rows)
-                    at_col = lax.rem(lax.rem(link, full_cols) - base_col + full_cols, full_cols)
-                    total = total + lax.dot_general(
-                        c[number - 1][jnp.minimum(at_row, coarse.nz + 1), jnp.minimum(at_col, coarse.ny + 1)],
-                        b[number][i, j, k],
-                        (((1,), (1,)), ((), ())),
-                        preferred_element_type=jnp.float32,
-                    )
+                    at_row = modulo(link // coarse.total_y - base_row, coarse.nz * peers_z)
+                    at_col = modulo(link - base_col, coarse.total_y)
+                    at = jnp.minimum(at_row, coarse.nz + 1) * (coarse.ny + 2) + jnp.minimum(at_col, coarse.ny + 1)
+                    lines[number][(i * level.ny + j) * 2 + k] = at
+            return carry
+
+        lax.fori_loop(0, level.nz, row, 0)
+
+    def prolong(number):
+        level = levels[number]
+
+        def row(i, carry):
+            for j in range(level.ny):
+                at = (i * level.ny + j) * 2
+                picked = [c_flat[number - 1][lines[number][at + k]] for k in range(2)]
+                total = g[number][i, j] + lax.dot_general(
+                    jnp.concatenate(picked, axis=1),
+                    jnp.concatenate([b[number][i, j, 0], b[number][i, j, 1]], axis=1),
+                    (((1,), (1,)), ((), ())),
+                    preferred_element_type=jnp.float32,
+                )
                 u[number][level.halo + i, level.off + j] = total
             return carry
 
         lax.fori_loop(0, level.nz, row, 0)
 
+    for number in range(1, n):
+        index_lines(number)
     for key in (("f", 0), ("t", 0), ("g", 0)):
         loads[key].wait()
     pl.semaphore_wait(barrier, len(partners))
@@ -306,7 +319,8 @@
     scratch += [pltpu.VMEM(x.shape, f32) for x in guess[1:]]
     scratch += [pltpu.VMEM(x.shape, bf16) for x in blocks]
     scratch += [pltpu.VMEM((l.nz + 2, l.ny + 2, sides, line), bf16) for l in levels[:-1]]
-    scratch += [pltpu.VMEM((l.nz + 2 * l.ring, l.ny, sides, line), f32) for l in levels]
+    scratch += [pltpu.VMEM((l.nz + 2 * l.ring, len(l.cols_of_ring), sides, line), f32) for l in levels]
+    scratch += [pltpu.SMEM((2 * l.nz * l.ny,), jnp.int32) for l in levels[1:]]
     scratch += [
         pltpu.SemaphoreType.DMA((3 * n + 2 * (n - 1),)),
         pltpu.SemaphoreType.DMA((n,)),

time: 73.4 us -> 68.3 us (0.931)
  Pallas kernels: 66.3 us -> 61.2 us
    pallas_call x1, Pallas kernels: 66.3 us -> 61.2 us  [shards(): pl.pallas_call(functools.partial(kernel, levels, table, peers), out_shape...]
where the time goes in v1:
time: 68.3 us; the launch traced here: 68 us
  Pallas kernels  61.2 us (90%)
  local copies, waits for them, and re-layouts  6.1 us (9%)
    pallas_call x1, Pallas kernels, shards(): pl.pallas_call(functools.partial(kernel, levels, table, peers), out_shape...  61.2 us
    unnamed x4, local copies, waits for them, and re-layouts  6.1 us

profile of v1, /device:TPU:1, one launch (start us, length us, event | category | flops | bytes accessed | tf_op | source)
XLA Modules:
  0.0 68.0 jit_solution(12428764330140987918)
XLA Ops:
  0.6 61.2 %shard_map.201 = (f32[1,1,16,128]{3,2,1,0:T(8,128)}, f32[2,2,16,128]{3,2,1,0:T(8,128)}, f32[4,4,16,128]{3,2,1,0:T(8,128)}, f32[8,8,16,128]{3,2,1,0:T(8,128)}) custom-call(f32[1,1,16,128]{3,2,1,0:T(8,128)} %refs_0_.1, f32[2,2,16,128]{3,2,1,0:T(8,128)} %refs_1_.1, f32[4,4,16,128]{3,2,1,0:T(8,128)} %refs_2_.1, f32[8,8,16,128]{3,2,1,0:T(8,128)} %refs_3_.1, ...), custom_call_target="tpu_custom_call" | custom-call | tf_op jit(solution)/shard_map/pallas_call | solution.py:331
  61.8 1.9 %copy.26 = f32[8,8,16,128]{3,2,1,0:T(8,128)} copy(f32[8,8,16,128]{3,2,1,0:T(8,128)} %get-tuple-element.16) | data formatting | bytes 1048576
  63.7 1.6 %copy.27 = f32[4,4,16,128]{3,2,1,0:T(8,128)} copy(f32[4,4,16,128]{3,2,1,0:T(8,128)} %get-tuple-element.17) | data formatting | bytes 262144
  65.3 1.4 %copy.28 = f32[2,2,16,128]{3,2,1,0:T(8,128)} copy(f32[2,2,16,128]{3,2,1,0:T(8,128)} %get-tuple-element.18) | data formatting | bytes 65536
  66.7 1.3 %copy.29 = f32[1,1,16,128]{3,2,1,0:T(8,128)} copy(f32[1,1,16,128]{3,2,1,0:T(8,128)} %get-tuple-element.19) | data formatting | bytes 16384

commit v2 on v1

--- a/solution.py
+++ b/solution.py
@@ -21,9 +21,10 @@
 A3, B3 = FACTOR_2 * FACTOR_1, 2.0 * FACTOR_2 / HALF
 
 RADIUS = 3
-RINGS = (0, 0, 0, 0)
-STRAIGHT = 40
-ROWS = 2
+RINGS = (0, 1, 0, 0)
+STRAIGHT = 64
+PIECE = 4
+ROWS = 5
 
 
 class Level:
@@ -36,7 +37,6 @@
         self.rows = nz + 2 * self.halo
         self.cols = self.total_y if self.full else ny + 2 * self.halo
         self.off = 0 if self.full else self.halo
-        self.cols_of_ring = sorted({self.col(y) for y in range(-ring, ny + ring)})
 
     def col(self, y):
         return y % self.total_y if self.full else y + self.off
@@ -68,8 +68,9 @@
                     else:
                         spans.append([i, span, 1])
                 for i, (j, count), rows in spans:
-                    found.append((oz, oy, i, j, rows, count))
-        return found
+                    for part in range(i, i + rows, PIECE):
+                        found.append((oz, oy, part, j, min(PIECE, i + rows - part), count))
+        return sorted(found, key=lambda m: -abs(m[1]))
 
 
 def ring_messages(nz, ny):
@@ -113,9 +114,8 @@
     u, f, t, d1, d2 = (refs[k * n : (k + 1) * n] for k in range(5))
     refs = refs[5 * n :]
     g, b, c = (None,) + refs[: n - 1], (None,) + refs[n - 1 : 2 * n - 2], refs[2 * n - 2 : 3 * n - 3]
-    result = refs[3 * n - 3 : 4 * n - 3]
-    lines, refs = (None,) + refs[4 * n - 3 : 5 * n - 4], refs[5 * n - 4 :]
-    local_sem, out_sem, send_sem, recv_sem = refs
+    lines, link_lines = (None,) + refs[3 * n - 3 : 4 * n - 4], (None,) + refs[4 * n - 4 : 5 * n - 5]
+    local_sem, send_sem, recv_sem = refs[5 * n - 5 :]
     c_flat = [x.reshape((-1,) + x.shape[2:]) for x in c]
 
     peers_z, peers_y = peers
@@ -142,6 +142,7 @@
         if number == 0:
             load(("g", 0), guess[0], u[0].at[own])
     for number in range(1, n):
+        load(("l", number), links[number], link_lines[number])
         load(("g", number), guess[number], g[number])
         load(("b", number), blocks[number], b[number])
 
@@ -167,9 +168,9 @@
             device_id_type=MESH,
         )
 
-    def send(kind, number):
-        for index, (k, l, _) in enumerate(table):
-            if (k, l) == (kind, number):
+    def send(kind, number, end=None):
+        for index, (k, l, m) in enumerate(table):
+            if (k, l) == (kind, number) and (end is None or m[2] + m[4] == end):
                 copies[index] = describe(index)
                 copies[index].start()
 
@@ -181,7 +182,7 @@
     def sweep(level, ring, body, after=None):
         cols = sorted({level.col(y) for y in range(-ring, level.ny + ring)})
         first, count = level.halo - ring, level.nz + 2 * ring
-        step = count if count * len(cols) <= STRAIGHT else ROWS
+        step = count if count * len(cols) <= STRAIGHT else max(k for k in range(1, ROWS + 1) if count % k == 0)
 
         def rows(start):
             for z in range(step):
@@ -219,25 +220,16 @@
             finish(z, y, out)
 
         def finish(z, y, out):
-            result[number][z - level.halo + ring, level.cols_of_ring.index(y)] = out
+            row, col = z - level.halo, y - level.off
+            if ring == 0 or (0 <= row < level.nz and 0 <= col < level.ny):
+                outs[number][row, col] = out
             if number < n - 1:
-                at = (y - level.off + 1) % level.total_y if level.full else y - level.off + 1
-                c[number][z - level.halo + 1, at] = out.astype(jnp.bfloat16)
-
-        def copy_out(start, rows):
-            at = start - level.halo
-            own = result[number].at[pl.ds(at, rows)]
-            pltpu.make_async_copy(own, outs[number].at[pl.ds(at, rows)], out_sem.at[number]).start()
+                at = (col + 1) % level.total_y if level.full else col + 1
+                c[number][row + 1, at] = out.astype(jnp.bfloat16)
 
         sweep(level, ring + 2, first)
         sweep(level, ring + 1, second)
-        sweep(level, ring, third, None if ring else copy_out)
-        own = result[number]
-        if ring:
-            own_cols = level.cols_of_ring.index(level.off)
-            own = own.at[pl.ds(ring, level.nz), pl.ds(own_cols, level.ny)]
-            pltpu.make_async_copy(own, outs[number], out_sem.at[number]).start()
-        return pltpu.make_async_copy(own, outs[number], out_sem.at[number])
+        sweep(level, ring, third)
 
     def index_lines(number):
         level, coarse = levels[number], levels[number - 1]
@@ -247,7 +239,7 @@
         def row(i, carry):
             for j in range(level.ny):
                 for k in range(2):
-                    link = links[number][(i, j, k) if level.ny == 2 else (i, k, j)]
+                    link = link_lines[number][(i, j, k) if level.ny == 2 else (i, k, j)]
                     at_row = modulo(link // coarse.total_y - base_row, coarse.nz * peers_z)
                     at_col = modulo(link - base_col, coarse.total_y)
                     at = jnp.minimum(at_row, coarse.nz + 1) * (coarse.ny + 2) + jnp.minimum(at_col, coarse.ny + 1)
@@ -272,35 +264,51 @@
                 u[number][level.halo + i, level.off + j] = total
             return carry
 
-        lax.fori_loop(0, level.nz, row, 0)
+        ends = sorted({m[2] + m[4] for k, l, m in table if (k, l) == ("u", number)} | {level.nz})
+        start = 0
+        for end in ends:
+            lax.fori_loop(start, end, row, 0)
+            send("u", number, end)
+            start = end
 
     for number in range(1, n):
+        loads[("l", number)].wait()
         index_lines(number)
     for key in (("f", 0), ("t", 0), ("g", 0)):
         loads[key].wait()
     pl.semaphore_wait(barrier, len(partners))
+    def send_inputs(number):
+        for kind in ("t", "f"):
+            loads[(kind, number)].wait()
+            send(kind, number)
+
     for kind in ("u", "f", "t"):
         send(kind, 0)
-    for number in range(1, n):
-        for kind in ("f", "t"):
-            loads[(kind, number)].wait()
-            send(kind, number)
-    outputs = []
+    send_inputs(1)
     for number in range(n):
         if number:
             loads[("g", number)].wait()
             loads[("b", number)].wait()
             prolong(number)
-            send("u", number)
+            if number == 1:
+                send_inputs(3)
         for kind in ("f", "t", "u"):
             receive(kind, number)
-        outputs.append(smooth(number))
-        if number < n - 1 and levels[number].ring == 0:
-            send("c", number)
-            receive("c", number)
+        smooth(number)
+        send("c", number)
+        if number == 0:
+            send_inputs(2)
+        receive("c", number)
     for index in range(len(table)):
         copies[index].wait_send()
-    for copy in outputs:
+
+
+def copy_out(*refs):
+    results, outs, sem = refs[: len(refs) // 2], refs[len(refs) // 2 : -1], refs[-1]
+    copies = [pltpu.make_async_copy(r, o, sem.at[k]) for k, (r, o) in enumerate(zip(results, outs))]
+    for copy in copies:
+        copy.start()
+    for copy in copies:
         copy.wait()
 
 
@@ -319,25 +327,34 @@
     scratch += [pltpu.VMEM(x.shape, f32) for x in guess[1:]]
     scratch += [pltpu.VMEM(x.shape, bf16) for x in blocks]
     scratch += [pltpu.VMEM((l.nz + 2, l.ny + 2, sides, line), bf16) for l in levels[:-1]]
-    scratch += [pltpu.VMEM((l.nz + 2 * l.ring, len(l.cols_of_ring), sides, line), f32) for l in levels]
     scratch += [pltpu.SMEM((2 * l.nz * l.ny,), jnp.int32) for l in levels[1:]]
+    scratch += [pltpu.SMEM(x.shape, jnp.int32) for x in links]
     scratch += [
-        pltpu.SemaphoreType.DMA((3 * n + 2 * (n - 1),)),
-        pltpu.SemaphoreType.DMA((n,)),
+        pltpu.SemaphoreType.DMA((3 * n + 3 * (n - 1),)),
         pltpu.SemaphoreType.DMA((len(table),)),
         pltpu.SemaphoreType.DMA((len(table),)),
     ]
-    hbm = pl.BlockSpec(memory_space=pltpu.HBM)
+    hbm, vmem = pl.BlockSpec(memory_space=pltpu.HBM), pl.BlockSpec(memory_space=pltpu.VMEM)
+    operands = [pltpu.with_memory_space_constraint(x, pltpu.HBM) for x in (*source, *guess, *shift, *blocks, *links)]
+    shapes = [jax.ShapeDtypeStruct(x.shape, f32) for x in source]
     results = pl.pallas_call(
         functools.partial(kernel, levels, table, peers),
-        out_shape=[jax.ShapeDtypeStruct(x.shape, f32) for x in source],
-        in_specs=[hbm] * (3 * n + len(blocks)) + [pl.BlockSpec(memory_space=pltpu.SMEM)] * len(links),
-        out_specs=[hbm] * n,
+        out_shape=shapes,
+        in_specs=[hbm] * len(operands),
+        out_specs=[vmem] * n,
         scratch_shapes=scratch,
         compiler_params=pltpu.CompilerParams(
-            collective_id=0, has_side_effects=True, vmem_limit_bytes=67043328
+            collective_id=0, has_side_effects=True, vmem_limit_bytes=32 * 1024 * 1024
         ),
-    )(*source, *guess, *shift, *blocks, *links)
+    )(*operands)
+    results = pl.pallas_call(
+        copy_out,
+        out_shape=shapes,
+        in_specs=[pl.BlockSpec(memory_space=pl.ANY)] * n,
+        out_specs=[hbm] * n,
+        scratch_shapes=[pltpu.SemaphoreType.DMA((n,))],
+        compiler_params=pltpu.CompilerParams(vmem_limit_bytes=2 * 1024 * 1024),
+    )(*results)
     return tuple(results[::-1])
 
 

time: 68.3 us -> 55.3 us (0.81)
  Pallas kernels: 61.2 us -> 54.5 us
  local copies, waits for them, and re-layouts: 6.1 us -> 0 us
    pallas_call x1, Pallas kernels: 61.2 us -> 53.6 us  [shards(): pl.pallas_call(functools.partial(kernel, levels, table, peers), out_shape...]
    unnamed x4 -> x0, local copies, waits for them, and re-layouts: 6.1 us -> none
    pallas_call x0 -> x1, Pallas kernels: none -> 0.89 us  [shards(): pl.pallas_call(copy_out, out_shape=shapes, in_specs=[pl.BlockSpec(memory_...]
where the time goes in v2:
time: 55.3 us; the launch traced here: 55.2 us
  Pallas kernels  54.5 us (99%)
  between operations  0.65 us (1%)
    pallas_call x1, Pallas kernels, shards(): pl.pallas_call(functools.partial(kernel, levels, table, peers), out_shape...  53.6 us

profile of v2, /device:TPU:1, one launch (start us, length us, event | category | flops | bytes accessed | tf_op | source)
XLA Modules:
  0.0 55.2 jit_solution(9651739981906757400)
XLA Ops:
  0.6 53.6 %shard_map.201 = (f32[1,1,16,128]{3,2,1,0:T(8,128)S(1)}, f32[2,2,16,128]{3,2,1,0:T(8,128)S(1)}, f32[4,4,16,128]{3,2,1,0:T(8,128)S(1)}, f32[8,8,16,128]{3,2,1,0:T(8,128)S(1)}) custom-call(f32[1,1,16,128]{3,2,1,0:T(8,128)} %refs_0_.1, f32[2,2,16,128]{3,2,1,0:T(8,128)} %refs_1_.1, f32[4,4,16,128]{3,2,1,0:T(8,128)} %refs_2_.1, f32[8,8,16,128]{3,2,1,0:T(8,128)} %refs_3_.1, ...), custom_call_target="tpu_custom_call" | custom-call | tf_op jit(solution)/shard_map/pallas_call | solution.py:340
  54.3 0.9 %shard_map.202 = (f32[1,1,16,128]{3,2,1,0:T(8,128)}, f32[2,2,16,128]{3,2,1,0:T(8,128)}, f32[4,4,16,128]{3,2,1,0:T(8,128)}, f32[8,8,16,128]{3,2,1,0:T(8,128)}) custom-call(f32[1,1,16,128]{3,2,1,0:T(8,128)S(1)} %get-tuple-element.12.refs_0_, f32[2,2,16,128]{3,2,1,0:T(8,128)S(1)} %get-tuple-element.13.refs_1_, f32[4,4,16,128]{3,2,1,0:T(8,128)S(1)} %get-tuple-element.14.refs_2_, ...), custom_call_target="tpu_custom_call" | custom-call | tf_op jit(solution)/shard_map/pallas_call | solution.py:350

commit v3 on v2

--- a/solution.py
+++ b/solution.py
@@ -23,6 +23,7 @@
 RADIUS = 3
 RINGS = (0, 1, 0, 0)
 STRAIGHT = 64
+PROLONG_ROWS = 2
 PIECE = 4
 ROWS = 5
 
@@ -96,6 +97,15 @@
     return levels, table
 
 
+def groups_of(table):
+    return sorted({(kind, number) for kind, number, _ in table})
+
+
+def group_lines(table, group):
+    lines = {"u": 16, "f": 16, "t": 1, "c": 8}[group[0]]
+    return sum(lines * m[4] * m[5] for kind, number, m in table if (kind, number) == group)
+
+
 def modulo(value, size):
     return (value + size) & (size - 1) if size & (size - 1) == 0 else lax.rem(value + size, size)
 
@@ -115,7 +125,7 @@
     refs = refs[5 * n :]
     g, b, c = (None,) + refs[: n - 1], (None,) + refs[n - 1 : 2 * n - 2], refs[2 * n - 2 : 3 * n - 3]
     lines, link_lines = (None,) + refs[3 * n - 3 : 4 * n - 4], (None,) + refs[4 * n - 4 : 5 * n - 5]
-    local_sem, send_sem, recv_sem = refs[5 * n - 5 :]
+    sizer, local_sem, send_sem, recv_sem = refs[5 * n - 5 :]
     c_flat = [x.reshape((-1,) + x.shape[2:]) for x in c]
 
     peers_z, peers_y = peers
@@ -147,7 +157,7 @@
         load(("b", number), blocks[number], b[number])
 
     buffers = {"u": u, "f": f, "t": t, "c": c}
-    copies = {}
+    groups = groups_of(table)
 
     def describe(index):
         kind, number, (oz, oy, i, j, rows, count) = table[index]
@@ -162,8 +172,8 @@
         return pltpu.make_async_remote_copy(
             src_ref=ref.at[source_at],
             dst_ref=ref.at[target_at],
-            send_sem=send_sem.at[index],
-            recv_sem=recv_sem.at[index],
+            send_sem=send_sem.at[groups.index((kind, number))],
+            recv_sem=recv_sem.at[groups.index((kind, number))],
             device_id=peer(oz, oy),
             device_id_type=MESH,
         )
@@ -171,13 +181,18 @@
     def send(kind, number, end=None):
         for index, (k, l, m) in enumerate(table):
             if (k, l) == (kind, number) and (end is None or m[2] + m[4] == end):
-                copies[index] = describe(index)
-                copies[index].start()
+                describe(index).start()
+
+    def whole(group):
+        size, place = group_lines(table, group), groups.index(group)
+        every = sizer.at[pl.ds(0, size)]
+        return pltpu.make_async_remote_copy(
+            every, every, send_sem.at[place], recv_sem.at[place], device_id=peer(0, 1), device_id_type=MESH
+        )
 
     def receive(kind, number):
-        for index, (k, l, _) in enumerate(table):
-            if (k, l) == (kind, number):
-                copies[index].wait_recv()
+        if (kind, number) in groups:
+            whole((kind, number)).wait_recv()
 
     def sweep(level, ring, body, after=None):
         cols = sorted({level.col(y) for y in range(-ring, level.ny + ring)})
@@ -267,13 +282,17 @@
         ends = sorted({m[2] + m[4] for k, l, m in table if (k, l) == ("u", number)} | {level.nz})
         start = 0
         for end in ends:
-            lax.fori_loop(start, end, row, 0)
+            step = max(k for k in range(1, PROLONG_ROWS + 1) if (end - start) % k == 0)
+
+            def some(i, carry, start=start, step=step):
+                for k in range(step):
+                    row(start + i * step + k, carry)
+                return carry
+
+            lax.fori_loop(0, (end - start) // step, some, 0)
             send("u", number, end)
             start = end
 
-    for number in range(1, n):
-        loads[("l", number)].wait()
-        index_lines(number)
     for key in (("f", 0), ("t", 0), ("g", 0)):
         loads[key].wait()
     pl.semaphore_wait(barrier, len(partners))
@@ -285,6 +304,9 @@
     for kind in ("u", "f", "t"):
         send(kind, 0)
     send_inputs(1)
+    for number in range(1, n):
+        loads[("l", number)].wait()
+        index_lines(number)
     for number in range(n):
         if number:
             loads[("g", number)].wait()
@@ -299,8 +321,8 @@
         if number == 0:
             send_inputs(2)
         receive("c", number)
-    for index in range(len(table)):
-        copies[index].wait_send()
+    for group in groups:
+        whole(group).wait_send()
 
 
 def copy_out(*refs):
@@ -330,9 +352,10 @@
     scratch += [pltpu.SMEM((2 * l.nz * l.ny,), jnp.int32) for l in levels[1:]]
     scratch += [pltpu.SMEM(x.shape, jnp.int32) for x in links]
     scratch += [
+        pltpu.VMEM((max(group_lines(table, group) for group in groups_of(table)), 1, line), f32),
         pltpu.SemaphoreType.DMA((3 * n + 3 * (n - 1),)),
-        pltpu.SemaphoreType.DMA((len(table),)),
-        pltpu.SemaphoreType.DMA((len(table),)),
+        pltpu.SemaphoreType.DMA((len(groups_of(table)),)),
+        pltpu.SemaphoreType.DMA((len(groups_of(table)),)),
     ]
     hbm, vmem = pl.BlockSpec(memory_space=pltpu.HBM), pl.BlockSpec(memory_space=pltpu.VMEM)
     operands = [pltpu.with_memory_space_constraint(x, pltpu.HBM) for x in (*source, *guess, *shift, *blocks, *links)]

time: 55.3 us -> 52.1 us (0.942)
  Pallas kernels: 54.5 us -> 51.3 us
    pallas_call x1, Pallas kernels: 53.6 us -> 50.4 us  [shards(): pl.pallas_call(functools.partial(kernel, levels, table, peers), out_shape...]
where the time goes in v3:
time: 52.1 us; the launch traced here: 51.9 us
  Pallas kernels  51.3 us (98%)
  between operations  0.65 us (1%)
    pallas_call x1, Pallas kernels, shards(): pl.pallas_call(functools.partial(kernel, levels, table, peers), out_shape...  50.4 us

profile of v3, /device:TPU:1, one launch (start us, length us, event | category | flops | bytes accessed | tf_op | source)
XLA Modules:
  0.0 51.9 jit_solution(17293728022200613608)
XLA Ops:
  0.6 50.4 %shard_map.201 = (f32[1,1,16,128]{3,2,1,0:T(8,128)S(1)}, f32[2,2,16,128]{3,2,1,0:T(8,128)S(1)}, f32[4,4,16,128]{3,2,1,0:T(8,128)S(1)}, f32[8,8,16,128]{3,2,1,0:T(8,128)S(1)}) custom-call(f32[1,1,16,128]{3,2,1,0:T(8,128)} %refs_0_.1, f32[2,2,16,128]{3,2,1,0:T(8,128)} %refs_1_.1, f32[4,4,16,128]{3,2,1,0:T(8,128)} %refs_2_.1, f32[8,8,16,128]{3,2,1,0:T(8,128)} %refs_3_.1, ...), custom_call_target="tpu_custom_call" | custom-call | tf_op jit(solution)/shard_map/pallas_call | solution.py:363
  51.0 0.9 %shard_map.202 = (f32[1,1,16,128]{3,2,1,0:T(8,128)}, f32[2,2,16,128]{3,2,1,0:T(8,128)}, f32[4,4,16,128]{3,2,1,0:T(8,128)}, f32[8,8,16,128]{3,2,1,0:T(8,128)}) custom-call(f32[1,1,16,128]{3,2,1,0:T(8,128)S(1)} %get-tuple-element.12.refs_0_, f32[2,2,16,128]{3,2,1,0:T(8,128)S(1)} %get-tuple-element.13.refs_1_, f32[4,4,16,128]{3,2,1,0:T(8,128)S(1)} %get-tuple-element.14.refs_2_, ...), custom_call_target="tpu_custom_call" | custom-call | tf_op jit(solution)/shard_map/pallas_call | solution.py:373

commit v4 on v3

--- a/solution.py
+++ b/solution.py
@@ -21,10 +21,12 @@
 A3, B3 = FACTOR_2 * FACTOR_1, 2.0 * FACTOR_2 / HALF
 
 RADIUS = 3
-RINGS = (0, 1, 0, 0)
+RINGS = (0, 1, 1, 0)
+NARROW = (False, True, True, True)
+NARROW_SOURCE = (True, True, True, True)
 STRAIGHT = 64
 PROLONG_ROWS = 2
-PIECE = 4
+PIECE = 2
 ROWS = 5
 
 
@@ -42,15 +44,19 @@
     def col(self, y):
         return y % self.total_y if self.full else y + self.off
 
-    def needed(self, z, y, radius):
-        def gap(p, n):
-            return max(0, -p - self.ring, p - (n - 1) - self.ring)
+    def gap(self, z, y, ring):
+        def along(p, n):
+            return max(0, -p - ring, p - (n - 1) - ring)
 
         turns = (-1, 0, 1) if self.full else (0,)
-        gap_y = min(gap(y + t * self.total_y, self.ny) for t in turns)
-        return gap(z, self.nz) + gap_y <= radius
-
-    def messages(self, radius):
+        return along(z, self.nz), min(along(y + t * self.total_y, self.ny) for t in turns)
+
+    def needs(self, z, y, radius, near):
+        if sum(self.gap(z, y, self.ring)) > radius:
+            return False
+        return near is None or near == (max(self.gap(z, y, 0)) == 1)
+
+    def messages(self, radius, near=None):
         found = []
         reach = -(-self.halo // self.nz)
         offsets_y = range(-(self.peers_y // 2 - 1), self.peers_y // 2 + 1) if self.full else range(-1, 2)
@@ -60,11 +66,12 @@
                     continue
                 spans = []
                 for i in range(self.nz):
-                    js = [j for j in range(self.ny) if self.needed(i - oz * self.nz, j - oy * self.ny, radius)]
+                    js = [j for j in range(self.ny) if self.needs(i - oz * self.nz, j - oy * self.ny, radius, near)]
                     if not js:
                         continue
+                    assert js == list(range(js[0], js[-1] + 1))
                     span = (js[0], len(js))
-                    if spans and spans[-1][1] == span:
+                    if spans and spans[-1][1] == span and spans[-1][0] + spans[-1][2] == i:
                         spans[-1][2] += 1
                     else:
                         spans.append([i, span, 1])
@@ -72,6 +79,16 @@
                     for part in range(i, i + rows, PIECE):
                         found.append((oz, oy, part, j, min(PIECE, i + rows - part), count))
         return sorted(found, key=lambda m: -abs(m[1]))
+
+    def far_cells(self, radius):
+        return sorted(
+            {
+                (self.halo + i + a - oz * self.nz, self.col(j + k - oy * self.ny))
+                for oz, oy, i, j, rows, count in self.messages(radius, False)
+                for a in range(rows)
+                for k in range(count)
+            }
+        )
 
 
 def ring_messages(nz, ny):
@@ -90,8 +107,11 @@
     levels = [Level(nz, ny, peers_z, peers_y, ring) for (nz, ny), ring in zip(shapes, RINGS)]
     table = []
     for number, level in enumerate(levels):
-        for kind, radius in (("u", RADIUS), ("f", RADIUS - 1), ("t", RADIUS - 1)):
-            table += [(kind, number, m) for m in level.messages(radius)]
+        for wide, narrow, radius, split in (("u", "v", RADIUS, NARROW[number]), ("f", "w", RADIUS - 1, NARROW_SOURCE[number])):
+            table += [(wide, number, m) for m in level.messages(radius, True if split else None)]
+            if split:
+                table += [(narrow, number, m) for m in level.messages(radius, False)]
+        table += [("t", number, m) for m in level.messages(RADIUS - 1)]
         if number < len(levels) - 1 and level.ring == 0:
             table += [("c", number, m) for m in ring_messages(level.nz, level.ny)]
     return levels, table
@@ -102,7 +122,7 @@
 
 
 def group_lines(table, group):
-    lines = {"u": 16, "f": 16, "t": 1, "c": 8}[group[0]]
+    lines = {"u": 16, "v": 8, "f": 16, "w": 8, "t": 1, "c": 8}[group[0]]
     return sum(lines * m[4] * m[5] for kind, number, m in table if (kind, number) == group)
 
 
@@ -125,7 +145,8 @@
     refs = refs[5 * n :]
     g, b, c = (None,) + refs[: n - 1], (None,) + refs[n - 1 : 2 * n - 2], refs[2 * n - 2 : 3 * n - 3]
     lines, link_lines = (None,) + refs[3 * n - 3 : 4 * n - 4], (None,) + refs[4 * n - 4 : 5 * n - 5]
-    sizer, local_sem, send_sem, recv_sem = refs[5 * n - 5 :]
+    v, w = refs[5 * n - 5 : 6 * n - 5], refs[6 * n - 5 : 7 * n - 5]
+    sizer, local_sem, send_sem, recv_sem = refs[7 * n - 5 :]
     c_flat = [x.reshape((-1,) + x.shape[2:]) for x in c]
 
     peers_z, peers_y = peers
@@ -156,7 +177,7 @@
         load(("g", number), guess[number], g[number])
         load(("b", number), blocks[number], b[number])
 
-    buffers = {"u": u, "f": f, "t": t, "c": c}
+    buffers = {"u": u, "v": v, "f": f, "w": w, "t": t, "c": c}
     groups = groups_of(table)
 
     def describe(index):
@@ -272,14 +293,16 @@
                 picked = [c_flat[number - 1][lines[number][at + k]] for k in range(2)]
                 total = g[number][i, j] + lax.dot_general(
                     jnp.concatenate(picked, axis=1),
-                    jnp.concatenate([b[number][i, j, 0], b[number][i, j, 1]], axis=1),
-                    (((1,), (1,)), ((), ())),
+                    jnp.concatenate([b[number][i, j, 0], b[number][i, j, 1]], axis=0),
+                    (((1,), (0,)), ((), ())),
                     preferred_element_type=jnp.float32,
                 )
                 u[number][level.halo + i, level.off + j] = total
+                if NARROW[number]:
+                    v[number][level.halo + i, level.off + j] = total.astype(jnp.bfloat16)
             return carry
 
-        ends = sorted({m[2] + m[4] for k, l, m in table if (k, l) == ("u", number)} | {level.nz})
+        ends = sorted({m[2] + m[4] for k, l, m in table if l == number and k in ("u", "v")} | {level.nz})
         start = 0
         for end in ends:
             step = max(k for k in range(1, PROLONG_ROWS + 1) if (end - start) % k == 0)
@@ -290,18 +313,50 @@
                 return carry
 
             lax.fori_loop(0, (end - start) // step, some, 0)
-            send("u", number, end)
+            for kind in ("v", "u"):
+                send(kind, number, end)
             start = end
 
     for key in (("f", 0), ("t", 0), ("g", 0)):
         loads[key].wait()
-    pl.semaphore_wait(barrier, len(partners))
+    def narrow_own(level, wide, narrow):
+        def row(i, carry):
+            for j in range(level.ny):
+                narrow[level.halo + i, level.off + j] = wide[level.halo + i, level.off + j].astype(jnp.bfloat16)
+            return carry
+
+        lax.fori_loop(0, level.nz, row, 0)
+
+    def widen_far(level, radius, narrow, wide):
+        for z, y in level.far_cells(radius):
+            wide[z, y] = narrow[z, y].astype(jnp.float32)
+
     def send_inputs(number):
         for kind in ("t", "f"):
             loads[(kind, number)].wait()
+        if NARROW_SOURCE[number]:
+            narrow_own(levels[number], f[number], w[number])
+        for kind in ("t", "w", "f"):
             send(kind, number)
 
-    for kind in ("u", "f", "t"):
+    def turn(number):
+        loads[("b", number)].wait()
+        level = levels[number]
+
+        def row(i, carry):
+            for j in range(level.ny):
+                for k in range(2):
+                    b[number][i, j, k] = b[number][i, j, k].T
+            return carry
+
+        lax.fori_loop(0, level.nz, row, 0)
+
+    if NARROW_SOURCE[0]:
+        narrow_own(levels[0], f[0], w[0])
+    if NARROW[0]:
+        narrow_own(levels[0], u[0], v[0])
+    pl.semaphore_wait(barrier, len(partners))
+    for kind in ("v", "w", "u", "f", "t"):
         send(kind, 0)
     send_inputs(1)
     for number in range(1, n):
@@ -310,16 +365,25 @@
     for number in range(n):
         if number:
             loads[("g", number)].wait()
-            loads[("b", number)].wait()
             prolong(number)
             if number == 1:
                 send_inputs(3)
-        for kind in ("f", "t", "u"):
+                turn(3)
+        else:
+            turn(1)
+        for kind in ("f", "w", "t"):
             receive(kind, number)
+        if NARROW_SOURCE[number]:
+            widen_far(levels[number], RADIUS - 1, w[number], f[number])
+        for kind in ("u", "v"):
+            receive(kind, number)
+        if NARROW[number]:
+            widen_far(levels[number], RADIUS, v[number], u[number])
         smooth(number)
         send("c", number)
         if number == 0:
             send_inputs(2)
+            turn(2)
         receive("c", number)
     for group in groups:
         whole(group).wait_send()
@@ -351,6 +415,7 @@
     scratch += [pltpu.VMEM((l.nz + 2, l.ny + 2, sides, line), bf16) for l in levels[:-1]]
     scratch += [pltpu.SMEM((2 * l.nz * l.ny,), jnp.int32) for l in levels[1:]]
     scratch += [pltpu.SMEM(x.shape, jnp.int32) for x in links]
+    scratch += [pltpu.VMEM((l.rows, l.cols, sides, line), bf16) for l in levels] * 2
     scratch += [
         pltpu.VMEM((max(group_lines(table, group) for group in groups_of(table)), 1, line), f32),
         pltpu.SemaphoreType.DMA((3 * n + 3 * (n - 1),)),

time: 52.1 us -> 45.9 us (0.88)
  Pallas kernels: 51.3 us -> 45.1 us
    pallas_call x1, Pallas kernels: 50.4 us -> 44.2 us  [shards(): pl.pallas_call(functools.partial(kernel, levels, table, peers), out_shape...]
where the time goes in v4:
time: 45.9 us; the launch traced here: 45.7 us
  Pallas kernels  45.1 us (98%)
  between operations  0.65 us (1%)
    pallas_call x1, Pallas kernels, shards(): pl.pallas_call(functools.partial(kernel, levels, table, peers), out_shape...  44.2 us

profile of v4, /device:TPU:1, one launch (start us, length us, event | category | flops | bytes accessed | tf_op | source)
XLA Modules:
  0.0 45.7 jit_solution(10720885619143110887)
XLA Ops:
  0.6 44.2 %shard_map.201 = (f32[1,1,16,128]{3,2,1,0:T(8,128)S(1)}, f32[2,2,16,128]{3,2,1,0:T(8,128)S(1)}, f32[4,4,16,128]{3,2,1,0:T(8,128)S(1)}, f32[8,8,16,128]{3,2,1,0:T(8,128)S(1)}) custom-call(f32[1,1,16,128]{3,2,1,0:T(8,128)} %refs_0_.1, f32[2,2,16,128]{3,2,1,0:T(8,128)} %refs_1_.1, f32[4,4,16,128]{3,2,1,0:T(8,128)} %refs_2_.1, f32[8,8,16,128]{3,2,1,0:T(8,128)} %refs_3_.1, ...), custom_call_target="tpu_custom_call" | custom-call | tf_op jit(solution)/shard_map/pallas_call | solution.py:428
  44.8 0.9 %shard_map.202 = (f32[1,1,16,128]{3,2,1,0:T(8,128)}, f32[2,2,16,128]{3,2,1,0:T(8,128)}, f32[4,4,16,128]{3,2,1,0:T(8,128)}, f32[8,8,16,128]{3,2,1,0:T(8,128)}) custom-call(f32[1,1,16,128]{3,2,1,0:T(8,128)S(1)} %get-tuple-element.12.refs_0_, f32[2,2,16,128]{3,2,1,0:T(8,128)S(1)} %get-tuple-element.13.refs_1_, f32[4,4,16,128]{3,2,1,0:T(8,128)S(1)} %get-tuple-element.14.refs_2_, ...), custom_call_target="tpu_custom_call" | custom-call | tf_op jit(solution)/shard_map/pallas_call | solution.py:438

commit v5 on v4

--- a/solution.py
+++ b/solution.py
@@ -126,6 +126,14 @@
     return sum(lines * m[4] * m[5] for kind, number, m in table if (kind, number) == group)
 
 
+def by_way(kind, number, message):
+    oz, oy, _, _, rows, count = message
+    return (-(abs(oy) + (abs(oz) + 1) // 2), rows * count)
+
+
+ORDER = by_way
+
+
 def modulo(value, size):
     return (value + size) & (size - 1) if size & (size - 1) == 0 else lax.rem(value + size, size)
 
@@ -199,10 +207,14 @@
             device_id_type=MESH,
         )
 
-    def send(kind, number, end=None):
-        for index, (k, l, m) in enumerate(table):
-            if (k, l) == (kind, number) and (end is None or m[2] + m[4] == end):
-                describe(index).start()
+    def send(kinds, number, end=None):
+        chosen = [
+            index
+            for index, (k, l, m) in enumerate(table)
+            if k in kinds and l == number and (end is None or m[2] + m[4] == end)
+        ]
+        for index in sorted(chosen, key=lambda index: ORDER(*table[index])):
+            describe(index).start()
 
     def whole(group):
         size, place = group_lines(table, group), groups.index(group)
@@ -313,8 +325,7 @@
                 return carry
 
             lax.fori_loop(0, (end - start) // step, some, 0)
-            for kind in ("v", "u"):
-                send(kind, number, end)
+            send("uv", number, end)
             start = end
 
     for key in (("f", 0), ("t", 0), ("g", 0)):
@@ -336,8 +347,7 @@
             loads[(kind, number)].wait()
         if NARROW_SOURCE[number]:
             narrow_own(levels[number], f[number], w[number])
-        for kind in ("t", "w", "f"):
-            send(kind, number)
+        send("twf", number)
 
     def turn(number):
         loads[("b", number)].wait()
@@ -356,8 +366,7 @@
     if NARROW[0]:
         narrow_own(levels[0], u[0], v[0])
     pl.semaphore_wait(barrier, len(partners))
-    for kind in ("v", "w", "u", "f", "t"):
-        send(kind, 0)
+    send("vwuft", 0)
     send_inputs(1)
     for number in range(1, n):
         loads[("l", number)].wait()

time: 45.9 us -> 45.2 us (0.985)
  Pallas kernels: 45.1 us -> 44.5 us
    pallas_call x1, Pallas kernels: 44.2 us -> 43.6 us  [shards(): pl.pallas_call(functools.partial(kernel, levels, table, peers), out_shape...]
where the time goes in v5:
time: 45.2 us; the launch traced here: 45.1 us
  Pallas kernels  44.5 us (98%)
  between operations  0.65 us (1%)
    pallas_call x1, Pallas kernels, shards(): pl.pallas_call(functools.partial(kernel, levels, table, peers), out_shape...  43.6 us

profile of v5, /device:TPU:1, one launch (start us, length us, event | category | flops | bytes accessed | tf_op | source)
XLA Modules:
  0.0 45.1 jit_solution(7658663189942844806)
XLA Ops:
  0.6 43.6 %shard_map.201 = (f32[1,1,16,128]{3,2,1,0:T(8,128)S(1)}, f32[2,2,16,128]{3,2,1,0:T(8,128)S(1)}, f32[4,4,16,128]{3,2,1,0:T(8,128)S(1)}, f32[8,8,16,128]{3,2,1,0:T(8,128)S(1)}) custom-call(f32[1,1,16,128]{3,2,1,0:T(8,128)} %refs_0_.1, f32[2,2,16,128]{3,2,1,0:T(8,128)} %refs_1_.1, f32[4,4,16,128]{3,2,1,0:T(8,128)} %refs_2_.1, f32[8,8,16,128]{3,2,1,0:T(8,128)} %refs_3_.1, ...), custom_call_target="tpu_custom_call" | custom-call | tf_op jit(solution)/shard_map/pallas_call | solution.py:437
  44.2 0.9 %shard_map.202 = (f32[1,1,16,128]{3,2,1,0:T(8,128)}, f32[2,2,16,128]{3,2,1,0:T(8,128)}, f32[4,4,16,128]{3,2,1,0:T(8,128)}, f32[8,8,16,128]{3,2,1,0:T(8,128)}) custom-call(f32[1,1,16,128]{3,2,1,0:T(8,128)S(1)} %get-tuple-element.12.refs_0_, f32[2,2,16,128]{3,2,1,0:T(8,128)S(1)} %get-tuple-element.13.refs_1_, f32[4,4,16,128]{3,2,1,0:T(8,128)S(1)} %get-tuple-element.14.refs_2_, ...), custom_call_target="tpu_custom_call" | custom-call | tf_op jit(solution)/shard_map/pallas_call | solution.py:447

commit v6 on v5

--- a/solution.py
+++ b/solution.py
@@ -24,7 +24,8 @@
 RINGS = (0, 1, 1, 0)
 NARROW = (False, True, True, True)
 NARROW_SOURCE = (True, True, True, True)
-STRAIGHT = 64
+STRAIGHT = 72
+EARLY = (False, False, False, True)
 PROLONG_ROWS = 2
 PIECE = 2
 ROWS = 5
@@ -227,29 +228,38 @@
         if (kind, number) in groups:
             whole((kind, number)).wait_recv()
 
-    def sweep(level, ring, body, after=None):
+    def sweep(level, ring, body, rows=None, done=0):
+        if done:
+            inner = (done, level.nz - done)
+            sweep(level, ring, body, (-ring, inner[0]))
+            sides = [*range(-ring, done), *range(level.ny - done, level.ny + ring)]
+            cells(level, body, inner, [level.col(y) for y in sides])
+            sweep(level, ring, body, (inner[1], level.nz + ring))
+            return
         cols = sorted({level.col(y) for y in range(-ring, level.ny + ring)})
-        first, count = level.halo - ring, level.nz + 2 * ring
+        cells(level, body, rows or (-ring, level.nz + ring), cols)
+
+    def cells(level, body, rows, cols):
+        first, count = level.halo + rows[0], rows[1] - rows[0]
         step = count if count * len(cols) <= STRAIGHT else max(k for k in range(1, ROWS + 1) if count % k == 0)
 
-        def rows(start):
+        def some(start):
             for z in range(step):
                 for y in cols:
                     body(start + z, y)
-            if after is not None:
-                after(start, step)
 
         if step == count:
-            rows(first)
+            some(first)
         else:
-            lax.fori_loop(0, count // step, lambda i, carry: (rows(first + i * step), carry)[1], 0)
+            lax.fori_loop(0, count // step, lambda i, carry: (some(first + i * step), carry)[1], 0)
 
     def beside(level, ref, z, y, middle):
         up, down = ((y + 1) % level.cols, (y - 1) % level.cols) if level.full else (y + 1, y - 1)
         return ref[z - 1, y] + ref[z + 1, y] + ref[z, up] + ref[z, down] + rolls(middle)
 
-    def smooth(number):
+    def smooth(number, early=False):
         level = levels[number]
+        done = 1 if EARLY[number] else 0
         uu, ff, tt, p, q = u[number], f[number], t[number], d1[number], d2[number]
         ring = level.ring
 
@@ -275,8 +285,12 @@
                 at = (col + 1) % level.total_y if level.full else col + 1
                 c[number][row + 1, at] = out.astype(jnp.bfloat16)
 
-        sweep(level, ring + 2, first)
-        sweep(level, ring + 1, second)
+        if early:
+            sweep(level, -1, first)
+            sweep(level, -2, second)
+            return
+        sweep(level, ring + 2, first, done=done)
+        sweep(level, ring + 1, second, done=2 * done)
         sweep(level, ring, third)
 
     def index_lines(number):
@@ -384,6 +398,8 @@
             receive(kind, number)
         if NARROW_SOURCE[number]:
             widen_far(levels[number], RADIUS - 1, w[number], f[number])
+        if EARLY[number]:
+            smooth(number, early=True)
         for kind in ("u", "v"):
             receive(kind, number)
         if NARROW[number]:

time: 45.2 us -> 44.8 us (level)
  Pallas kernels: 44.5 us -> 44 us
where the time goes in v6:
time: 44.8 us; the launch traced here: 44.6 us
  Pallas kernels  44 us (98%)
  between operations  0.65 us (1%)
    pallas_call x1, Pallas kernels, shards(): pl.pallas_call(functools.partial(kernel, levels, table, peers), out_shape...  43.1 us

profile of v6, /device:TPU:1, one launch (start us, length us, event | category | flops | bytes accessed | tf_op | source)
XLA Modules:
  0.0 44.6 jit_solution(2347764142179193715)
XLA Ops:
  0.6 43.1 %shard_map.201 = (f32[1,1,16,128]{3,2,1,0:T(8,128)S(1)}, f32[2,2,16,128]{3,2,1,0:T(8,128)S(1)}, f32[4,4,16,128]{3,2,1,0:T(8,128)S(1)}, f32[8,8,16,128]{3,2,1,0:T(8,128)S(1)}) custom-call(f32[1,1,16,128]{3,2,1,0:T(8,128)} %refs_0_.1, f32[2,2,16,128]{3,2,1,0:T(8,128)} %refs_1_.1, f32[4,4,16,128]{3,2,1,0:T(8,128)} %refs_2_.1, f32[8,8,16,128]{3,2,1,0:T(8,128)} %refs_3_.1, ...), custom_call_target="tpu_custom_call" | custom-call | tf_op jit(solution)/shard_map/pallas_call | solution.py:453
  43.8 0.9 %shard_map.202 = (f32[1,1,16,128]{3,2,1,0:T(8,128)}, f32[2,2,16,128]{3,2,1,0:T(8,128)}, f32[4,4,16,128]{3,2,1,0:T(8,128)}, f32[8,8,16,128]{3,2,1,0:T(8,128)}) custom-call(f32[1,1,16,128]{3,2,1,0:T(8,128)S(1)} %get-tuple-element.12.refs_0_, f32[2,2,16,128]{3,2,1,0:T(8,128)S(1)} %get-tuple-element.13.refs_1_, f32[4,4,16,128]{3,2,1,0:T(8,128)S(1)} %get-tuple-element.14.refs_2_, ...), custom_call_target="tpu_custom_call" | custom-call | tf_op jit(solution)/shard_map/pallas_call | solution.py:463
